TPU v7x, 32 devices: a whole 2x2x4 slice. The times are simulated.
32 devices in a mesh: wide: 8 (over z, core), narrow: 4 (over y, x).
Axes of the slice: x: 2, y: 2, z: 4, core: 2. Of those that a mesh axis runs over, the one named last changes fastest.
Arguments:
- points: float32 [8192, 128], P(('wide', 'narrow')), may hold values from -6 to 6
- targets: float32 [16, 8192], P(None, ('wide', 'narrow')), may hold values from -6 to 6
- start: float32 [16, 8192], P(None, ('wide', 'narrow')), may hold values from -6 to 6
- interp: float32 [8192, 128], P(('wide', 'narrow')), may hold values from -0.375 to 0.375
- skel_points: float32 [1024, 128], P('wide'), may hold values from -6 to 6
- near_leaves: int32 [64, 8], P(('wide', 'narrow')), may hold values from 0 to 7, as said below
- near_count: int32 [64], P(('wide', 'narrow')), may hold values from 1 to 8
Outputs:
- weights: float32 [16, 8192], P(None, ('wide', 'narrow'))
- residual: float32 [16, 8192], P(None, ('wide', 'narrow'))
Inputs may be any that keep to these rules, and one draw needn't show every extreme that they name: `near_leaves`: each row names 8 different leaves of the row's own subtree.
All inputs are finite; a program needn't handle non-finite values.
Results may differ from a plain program's by a relative error of at most 0.0003.
Values sent between devices are 32-bit elements; how exact they have to be, the bound alone decides.
No kernel may reach another device: no remote copies, remote signals or barrier semaphores. Data moves between devices by JAX's collectives and lax.ppermute only.
A program may use at most 64 MiB of HBM per device.

v0:
```python
import math
import jax
import jax.numpy as jnp
from jax import lax
from jax.sharding import PartitionSpec as P

ITERS = 2
ridge_shift = 1.0
step_size = 0.05
kernel_rate = 2.0
highest = lax.Precision.HIGHEST


def kernel(left_points, right_points, features):
    cross_prod = jnp.dot(
        left_points, right_points.T, precision=highest, preferred_element_type=jnp.float32
    )
    left_sq = jnp.sum(left_points * left_points, axis=1)
    right_sq = jnp.sum(right_points * right_points, axis=1)
    return jnp.exp(
        -(kernel_rate / features) * (left_sq[:, None] + right_sq[None, :] - 2.0 * cross_prod)
    )


def far_block(row_blocks, skeleton, columns, features):

    def row_group(block_points):
        kernel_vals = kernel(block_points, skeleton, features)
        return jnp.einsum("rs,ps->rp", columns, kernel_vals, precision=highest)

    pieces_out = lax.map(row_group, row_blocks)
    return jnp.transpose(pieces_out, (1, 0, 2)).reshape(columns.shape[0], -1)


def on_device(points, targets, start, interp, skel_points, near_leaves, near_count):
    leaf_dev, near_slots = near_leaves.shape
    row_total, features = points.shape
    leaf_size = row_total // leaf_dev
    rhs_count = targets.shape[0]
    skel_rank = interp.shape[1]
    block_rows = math.gcd(row_total, 512)
    row_blocks = points.reshape(row_total // block_rows, block_rows, features)
    own_blocks = points.reshape(leaf_dev, leaf_size, features)
    subtree = lax.all_gather(points, "narrow", axis=0, tiled=True).reshape(-1, leaf_size, features)
    neighbours = subtree[near_leaves]
    cross_prod = jnp.einsum("ipd,ikqd->ikpq", own_blocks, neighbours, precision=highest)
    own_sq = jnp.sum(own_blocks * own_blocks, axis=-1)
    near_sq = jnp.sum(neighbours * neighbours, axis=-1)
    live_mask = (jnp.arange(near_slots, dtype=jnp.int32)[None, :] < near_count[:, None]).astype(
        jnp.float32
    )
    distance = own_sq[:, None, :, None] + near_sq[:, :, None, :] - 2.0 * cross_prod
    near_kern = jnp.exp(-(kernel_rate / features) * distance) * live_mask[:, :, None, None]
    group_index = lax.axis_index("wide")
    weights = start
    residual = targets
    for iteration in range(ITERS):
        gathered = lax.all_gather(weights, "narrow", axis=1, tiled=True).reshape(
            rhs_count, -1, leaf_size
        )
        picked = gathered[:, near_leaves]
        near_term = jnp.einsum("ikpq,rikq->rip", near_kern, picked, precision=highest).reshape(
            rhs_count, row_total
        )
        node_local = jnp.dot(weights, interp, precision=highest, preferred_element_type=jnp.float32)
        summed = lax.psum(node_local, "narrow")
        skel_table = lax.all_gather(summed, "wide", axis=1, tiled=True)
        owner_node = jnp.arange(skel_table.shape[1], dtype=jnp.int32) // skel_rank
        skel_table = jnp.where((owner_node == group_index)[None, :], jnp.float32(0.0), skel_table)
        far_term = far_block(
            row_blocks,
            lax.all_gather(skel_points, "wide", axis=0, tiled=True),
            skel_table,
            features,
        )
        residual = targets - (ridge_shift * weights + (near_term + far_term))
        weights = weights + step_size * residual
    return (weights, residual)


def solution(mesh):
    in_specs = (
        P(("wide", "narrow"), None),
        P(None, ("wide", "narrow")),
        P(None, ("wide", "narrow")),
        P(("wide", "narrow"), None),
        P("wide", None),
        P(("wide", "narrow"), None),
        P(("wide", "narrow")),
    )
    out_specs = (P(None, ("wide", "narrow")), P(None, ("wide", "narrow")))
    return jax.shard_map(
        on_device, mesh=mesh, in_specs=in_specs, out_specs=out_specs, check_vma=False
    )
```

profile of v0, /device:TPU:0, one launch (start us, length us, event | category | flops | bytes accessed | tf_op | source)
XLA Modules:
  0.0 100.6 jit_solution(13071996611529464808)
XLA Ops:
  0.6 0.0 copy-start
  0.6 0.7 compare_select_fusion
  1.4 0.1 reshape.77
  1.5 11.9 %all_gather.20 = f32[1024,128]{1,0:T(8,128)S(1)} all-gather(f32[256,128]{1,0:T(8,128)} %param.7), channel_id=1, replica_groups=mesh['wide'=8,'narrow'=4] {'narrow'}, dimensions={0}, use_global_device_ids=true | all-gather | bytes 655360 | tf_op jit(solution)/shard_map/all_gather | solution.py:44
  13.3 0.6 gather_fusion.1
  13.9 0.0 copy-start.1
  14.0 0.3 multiply_reduce_fusion
  14.3 0.5 copy-done.1
  14.8 0.1 multiply_reduce_fusion.2
  15.0 0.0 copy-start.5
  15.0 0.6 copy-done.5
  15.6 0.1 compare_convert_fusion
  15.7 0.0 copy-start.2
  15.7 1.2 %fusion.7 = f32[2,8,128,128]{2,3,1,0:T(8,128)S(1)} fusion(f32[2,8,128,128]{3,2,1,0:T(8,128)S(1)} %bitcast.65, f32[2,128,128,1]{2,1,3,0:T(8,128)S(1)} %bitcast.67, f32[2,8]{1,0:T(2,128)S(1)} %compare_convert_fusion, f32[2,8,128]{2,1,0:T(8,128)S(1)} %multiply_reduce_fusion, f32[2,128]{1,0:T(2,128)S(1)} %bitcast.70), kind=kOutput, calls=%fused_computation.12 | convolution fusion | flops 403963904 | bytes 2237504 | tf_op jit(solution)/shard_map/ipd,ikqd->ikpq/dot_general | solution.py:46
  16.9 0.0 copy-done.2
  16.9 7.9 %all_gather.19 = f32[16,1024]{1,0:T(8,128)S(1)} all-gather(f32[16,256]{1,0:T(8,128)S(1)} %copy-done.2), channel_id=1, replica_groups=mesh['wide'=8,'narrow'=4] {'narrow'}, dimensions={1}, use_global_device_ids=true | all-gather | bytes 81920 | tf_op jit(solution)/shard_map/all_gather | solution.py:58
  24.8 0.6 gather_fusion
  25.4 0.0 copy-start.4
  25.4 0.6 convolution_bitcast_fusion.1
  26.0 0.2 copy-done.4
  26.2 15.2 %all_gather.22 = f32[1024,128]{1,0:T(8,128)S(1)} all-gather(f32[128,128]{1,0:T(8,128)S(1)} %copy-done.4), channel_id=1, replica_groups=mesh['wide'=8,'narrow'=4] {'wide'}, dimensions={0}, use_global_device_ids=true | all-gather | bytes 589824 | tf_op jit(solution)/shard_map/all_gather | solution.py:72
  41.4 0.2 multiply_reduce_fusion.1
  41.6 1.2 %fusion.2 = f32[256,1024]{1,0:T(8,128)S(1)} fusion(f32[256,128]{1,0:T(8,128)S(1)} %copy-done.1, f32[1024,128]{1,0:T(8,128)S(1)} %all_gather.22, f32[1024]{0:T(1024)S(1)} %multiply_reduce_fusion.1, f32[256]{0:T(256)S(1)} %multiply_reduce_fusion.2), kind=kOutput, calls=%fused_computation.6 | convolution fusion | flops 403701760 | bytes 1709056 | tf_op jit(solution)/shard_map/while/body/eval_jaxpr/dot_general | solution.py:15
  42.8 0.0 copy-done
  42.8 0.2 fusion.26
  43.0 9.1 %psum.14 = f32[16,128]{1,0:T(8,128)S(1)} all-reduce(f32[16,128]{1,0:T(8,128)S(1)} %fusion.26), channel_id=1, replica_groups=mesh['wide'=8,'narrow'=4] {'narrow'}, use_global_device_ids=true, to_apply=%region_2.0 | all-reduce | flops 2048 | bytes 16384 | tf_op jit(solution)/shard_map/psum | solution.py:66
  52.1 0.0 copy-start.3
  52.1 14.0 %all_gather.21 = f32[16,1024]{1,0:T(8,128)S(1)} all-gather(f32[16,128]{1,0:T(8,128)S(1)} %psum.14), channel_id=1, replica_groups=mesh['wide'=8,'narrow'=4] {'wide'}, dimensions={1}, use_global_device_ids=true | all-gather | bytes 73728 | tf_op jit(solution)/shard_map/all_gather | solution.py:67
  66.1 0.0 copy-done.3
  66.1 0.9 fusion.13
  67.0 7.6 %all_gather.23 = f32[16,1024]{1,0:T(8,128)S(1)} all-gather(f32[16,256]{1,0:T(8,128)S(1)} %fusion.13), channel_id=1, replica_groups=mesh['wide'=8,'narrow'=4] {'narrow'}, dimensions={1}, use_global_device_ids=true | all-gather | bytes 81920 | tf_op jit(solution)/shard_map/all_gather | solution.py:58
  74.6 0.6 gather_fusion.2
  75.2 0.6 convolution_bitcast_fusion
  75.8 0.2 fusion.27
  76.0 9.1 %psum.15 = f32[16,128]{1,0:T(8,128)S(1)} all-reduce(f32[16,128]{1,0:T(8,128)S(1)} %fusion.27), channel_id=1, replica_groups=mesh['wide'=8,'narrow'=4] {'narrow'}, use_global_device_ids=true, to_apply=%region_4.5 | all-reduce | flops 2048 | bytes 16384 | tf_op jit(solution)/shard_map/psum | solution.py:66
  85.1 14.0 %all_gather.24 = f32[16,1024]{1,0:T(8,128)S(1)} all-gather(f32[16,128]{1,0:T(8,128)S(1)} %psum.15), channel_id=1, replica_groups=mesh['wide'=8,'narrow'=4] {'wide'}, dimensions={1}, use_global_device_ids=true | all-gather | bytes 73728 | tf_op jit(solution)/shard_map/all_gather | solution.py:67
  99.0 1.5 %multiply_add_fusion = (f32[16,256]{1,0:T(8,128)}, f32[16,256]{1,0:T(8,128)}) fusion(f32[16,256]{1,0:T(8,128)S(1)} %fusion.13, f32[16,256]{1,0:T(8,128)S(1)} %copy-done.3, f32[256,1024]{1,0:T(8,128)S(1)} %fusion.2, f32[16,1024]{1,0:T(8,128)S(1)} %all_gather.24, pred[1024]{0:T(1024)(128)(4,1)S(1)} %fusion.20, f32[2,2,8,128]{3,2,1,0:T(8,128)S(1)} %convolution_bitcast_fusion), kind=kOutput, calls=%fused_computation.34 | convolution fusion | flops 50368512 | bytes 1197056 | tf_op jit(solution)/shard_map/while/body/eval_jaxpr/rs,ps->rp/dot_general | solution.py:29
  (4 shorter events, 0.0 us)
Async XLA Ops:
  0.6 42.2 %copy-start = (f32[256,128]{1,0:T(8,128)S(1)}, f32[256,128]{1,0:T(8,128)}, u32[]{:S(2)}) copy-start(f32[256,128]{1,0:T(8,128)} %param.10) | copy-start | bytes 393220
  13.9 0.9 copy-start.1
  15.0 0.7 copy-start.5
  15.7 1.2 %copy-start.2 = (f32[16,256]{1,0:T(8,128)S(1)}, f32[16,256]{1,0:T(8,128)}, u32[]{:S(2)}) copy-start(f32[16,256]{1,0:T(8,128)} %param.9) | copy-start | bytes 49156
  25.4 0.8 copy-start.4
  52.1 14.0 %copy-start.3 = (f32[16,256]{1,0:T(8,128)S(1)}, f32[16,256]{1,0:T(8,128)}, u32[]{:S(2)}) copy-start(f32[16,256]{1,0:T(8,128)} %param.8) | copy-start | bytes 49156
where the time goes:
time: 101 us
  blocking collectives  88.6 us (88%)
  matrix products  6.43 us (6%)
  local copies, waits for them, and re-layouts  3.27 us (3%)
  other arithmetic  1.46 us (1%)
    all_gather x2, blocking collectives, on_device(): skel_table = lax.all_gather(summed, 'wide', axis=1, tiled=True)  27.9 us
    psum x2, blocking collectives, on_device(): summed = lax.psum(node_local, 'narrow')  18.2 us
    all_gather x2, blocking collectives, on_device(): lax.all_gather(weights, 'narrow', axis=1, tiled=True)  15.5 us
    all_gather x1, blocking collectives, on_device(): lax.all_gather(skel_points, 'wide', axis=0, tiled=True)  15.2 us
    all_gather x1, blocking collectives, on_device(): lax.all_gather(points, 'narrow', axis=0, tiled=True)  11.9 us
    dot_general x2, matrix products, row_group(): return jnp.einsum('rs,ps->rp', columns, kernel_vals, precision=highest)  2.48 us

commit v1 on v0

--- a/solution.py
+++ b/solution.py
@@ -55,9 +55,11 @@
     weights = start
     residual = targets
     for iteration in range(ITERS):
-        gathered = lax.all_gather(weights, "narrow", axis=1, tiled=True).reshape(
-            rhs_count, -1, leaf_size
-        )
+
+        def _open_desk(at_axis, matrix):
+            return jnp.concatenate(jax.lax.all_gather(matrix, axis_name="narrow"), at_axis)
+
+        gathered = _open_desk(1, weights).reshape(rhs_count, -1, leaf_size)
         picked = gathered[:, near_leaves]
         near_term = jnp.einsum("ikpq,rikq->rip", near_kern, picked, precision=highest).reshape(
             rhs_count, row_total

time: 101 us -> 101 us (level)
  no operation moved by 1% of the time
where the time goes in v1:
time: 101 us
  blocking collectives  88.6 us (88%)
  matrix products  6.42 us (6%)
  local copies, waits for them, and re-layouts  3.43 us (3%)
  other arithmetic  1.46 us (1%)
    all_gather x2, blocking collectives, on_device(): skel_table = lax.all_gather(summed, 'wide', axis=1, tiled=True)  27.9 us
    psum x2, blocking collectives, on_device(): summed = lax.psum(node_local, 'narrow')  18.2 us
    all_gather x2, blocking collectives, _open_desk(): jax.lax.all_gather(matrix, axis_name='narrow')  15.5 us
    all_gather x1, blocking collectives, on_device(): lax.all_gather(skel_points, 'wide', axis=0, tiled=True)  15.2 us
    all_gather x1, blocking collectives, on_device(): lax.all_gather(points, 'narrow', axis=0, tiled=True)  11.9 us
    dot_general x2, matrix products, row_group(): return jnp.einsum('rs,ps->rp', columns, kernel_vals, precision=highest)  2.48 us

profile of v1, /device:TPU:0, one launch (start us, length us, event | category | flops | bytes accessed | tf_op | source)
XLA Modules:
  0.0 100.8 jit_solution(14994179904077761409)
XLA Ops:
  0.6 0.0 copy-start
  0.6 0.7 compare_select_fusion
  1.4 0.1 reshape.77
  1.5 11.9 %all_gather.27 = f32[1024,128]{1,0:T(8,128)S(1)} all-gather(f32[256,128]{1,0:T(8,128)} %param.7), channel_id=1, replica_groups=mesh['wide'=8,'narrow'=4] {'narrow'}, dimensions={0}, use_global_device_ids=true | all-gather | bytes 655360 | tf_op jit(solution)/shard_map/all_gather | solution.py:44
  13.3 0.6 gather_fusion.1
  13.9 0.0 copy-start.1
  14.0 0.3 multiply_reduce_fusion
  14.3 0.5 copy-done.1
  14.8 0.1 multiply_reduce_fusion.2
  15.0 0.0 copy-start.5
  15.0 0.6 copy-done.5
  15.6 0.1 compare_convert_fusion
  15.7 0.0 copy-start.2
  15.7 1.2 %fusion.7 = f32[2,8,128,128]{2,3,1,0:T(8,128)S(1)} fusion(f32[2,8,128,128]{3,2,1,0:T(8,128)S(1)} %bitcast.63, f32[2,128,128,1]{2,1,3,0:T(8,128)S(1)} %bitcast.65, f32[2,8]{1,0:T(2,128)S(1)} %compare_convert_fusion, f32[2,8,128]{2,1,0:T(8,128)S(1)} %multiply_reduce_fusion, f32[2,128]{1,0:T(2,128)S(1)} %bitcast.72), kind=kOutput, calls=%fused_computation.12 | convolution fusion | flops 403963904 | bytes 2237504 | tf_op jit(solution)/shard_map/ipd,ikqd->ikpq/dot_general | solution.py:46
  16.9 0.0 copy-done.2
  16.9 7.9 %all-gather = f32[64,256]{1,0:T(8,128)S(1)} all-gather(f32[16,256]{1,0:T(8,128)S(1)} %copy-done.2), channel_id=2, replica_groups=mesh['wide'=8,'narrow'=4] {'narrow'}, dimensions={0}, use_global_device_ids=true | all-gather | bytes 81920 | tf_op jit(solution)/shard_map/all_gather | solution.py:60
  24.9 0.6 gather_fusion
  25.5 0.0 copy-start.4
  25.5 0.6 convolution_bitcast_fusion.1
  26.1 0.2 copy-done.4
  26.3 15.2 %all_gather.29 = f32[1024,128]{1,0:T(8,128)S(1)} all-gather(f32[128,128]{1,0:T(8,128)S(1)} %copy-done.4), channel_id=1, replica_groups=mesh['wide'=8,'narrow'=4] {'wide'}, dimensions={0}, use_global_device_ids=true | all-gather | bytes 589824 | tf_op jit(solution)/shard_map/all_gather | solution.py:74
  41.5 0.2 multiply_reduce_fusion.1
  41.7 1.1 %fusion.2 = f32[256,1024]{1,0:T(8,128)S(1)} fusion(f32[256,128]{1,0:T(8,128)S(1)} %copy-done.1, f32[1024,128]{1,0:T(8,128)S(1)} %all_gather.29, f32[1024]{0:T(1024)S(1)} %multiply_reduce_fusion.1, f32[256]{0:T(256)S(1)} %multiply_reduce_fusion.2), kind=kOutput, calls=%fused_computation.6 | convolution fusion | flops 403701760 | bytes 1709056 | tf_op jit(solution)/shard_map/while/body/eval_jaxpr/dot_general | solution.py:15
  42.9 0.0 copy-done
  42.9 0.2 fusion.26
  43.1 9.1 %psum.14 = f32[16,128]{1,0:T(8,128)S(1)} all-reduce(f32[16,128]{1,0:T(8,128)S(1)} %fusion.26), channel_id=1, replica_groups=mesh['wide'=8,'narrow'=4] {'narrow'}, use_global_device_ids=true, to_apply=%region_2.0 | all-reduce | flops 2048 | bytes 16384 | tf_op jit(solution)/shard_map/psum | solution.py:68
  52.2 0.0 copy-start.3
  52.2 14.0 %all_gather.28 = f32[16,1024]{1,0:T(8,128)S(1)} all-gather(f32[16,128]{1,0:T(8,128)S(1)} %psum.14), channel_id=1, replica_groups=mesh['wide'=8,'narrow'=4] {'wide'}, dimensions={1}, use_global_device_ids=true | all-gather | bytes 73728 | tf_op jit(solution)/shard_map/all_gather | solution.py:69
  66.1 0.0 copy-done.3
  66.1 0.9 fusion.13
  67.1 7.6 %all-gather.1 = f32[64,256]{1,0:T(8,128)S(1)} all-gather(f32[16,256]{1,0:T(8,128)S(1)} %fusion.13), channel_id=3, replica_groups=mesh['wide'=8,'narrow'=4] {'narrow'}, dimensions={0}, use_global_device_ids=true | all-gather | bytes 81920 | tf_op jit(solution)/shard_map/all_gather | solution.py:60
  74.8 0.6 gather_fusion.2
  75.4 0.6 convolution_bitcast_fusion
  76.0 0.2 fusion.27
  76.2 9.1 %psum.15 = f32[16,128]{1,0:T(8,128)S(1)} all-reduce(f32[16,128]{1,0:T(8,128)S(1)} %fusion.27), channel_id=1, replica_groups=mesh['wide'=8,'narrow'=4] {'narrow'}, use_global_device_ids=true, to_apply=%region_4.5 | all-reduce | flops 2048 | bytes 16384 | tf_op jit(solution)/shard_map/psum | solution.py:68
  85.3 14.0 %all_gather.32 = f32[16,1024]{1,0:T(8,128)S(1)} all-gather(f32[16,128]{1,0:T(8,128)S(1)} %psum.15), channel_id=1, replica_groups=mesh['wide'=8,'narrow'=4] {'wide'}, dimensions={1}, use_global_device_ids=true | all-gather | bytes 73728 | tf_op jit(solution)/shard_map/all_gather | solution.py:69
  99.2 1.5 %multiply_add_fusion = (f32[16,256]{1,0:T(8,128)}, f32[16,256]{1,0:T(8,128)}) fusion(f32[16,256]{1,0:T(8,128)S(1)} %fusion.13, f32[16,256]{1,0:T(8,128)S(1)} %copy-done.3, f32[256,1024]{1,0:T(8,128)S(1)} %fusion.2, f32[16,1024]{1,0:T(8,128)S(1)} %all_gather.32, pred[1024]{0:T(1024)(128)(4,1)S(1)} %fusion.20, f32[2,2,8,128]{3,2,1,0:T(8,128)S(1)} %convolution_bitcast_fusion), kind=kOutput, calls=%fused_computation.34 | convolution fusion | flops 50368512 | bytes 1197056 | tf_op jit(solution)/shard_map/while/body/eval_jaxpr/rs,ps->rp/dot_general | solution.py:29
  (8 shorter events, 0.2 us)
Async XLA Ops:
  0.6 42.3 %copy-start = (f32[256,128]{1,0:T(8,128)S(1)}, f32[256,128]{1,0:T(8,128)}, u32[]{:S(2)}) copy-start(f32[256,128]{1,0:T(8,128)} %param.10) | copy-start | bytes 393220
  13.9 0.9 copy-start.1
  15.0 0.7 copy-start.5
  15.7 1.2 %copy-start.2 = (f32[16,256]{1,0:T(8,128)S(1)}, f32[16,256]{1,0:T(8,128)}, u32[]{:S(2)}) copy-start(f32[16,256]{1,0:T(8,128)} %param.9) | copy-start | bytes 49156
  25.5 0.8 copy-start.4
  52.2 14.0 %copy-start.3 = (f32[16,256]{1,0:T(8,128)S(1)}, f32[16,256]{1,0:T(8,128)}, u32[]{:S(2)}) copy-start(f32[16,256]{1,0:T(8,128)} %param.8) | copy-start | bytes 49156
